TPU v7x, 32 devices: a whole 2x2x4 slice. The times are simulated.
32 devices in a mesh: row: 8 (over z, y), col: 4 (over x, core).
Axes of the slice: x: 2, y: 2, z: 4, core: 2. Of those that a mesh axis runs over, the one named last changes fastest.
Arguments:
- matrix: float32 [4, 8, 512, 8, 4, 512], P(None, 'row', None, None, 'col'), may hold values from -30 to 30, as said below
Outputs:
- factored: float32 [4, 8, 512, 8, 4, 512], P(None, 'row', None, None, 'col')
Inputs may be any that keep to these rules, and one draw needn't show every extreme that they name: matrix is symmetric, positive definite and well conditioned.
All inputs are finite; a program needn't handle non-finite values.
Results may differ from a plain program's by a relative error of at most 0.00013.
Values sent between devices are 32-bit elements; how exact they have to be, the bound alone decides.
A program may use at most 192 MiB of HBM per device.

v0:
```python
import jax
import jax.numpy as jnp
from jax import lax
from jax.sharding import PartitionSpec as P

NB = 512
STEPS = 2


def spread(value, axis, source):
    kept = jnp.where(lax.axis_index(axis) == source, value, 0).astype(value.dtype)
    return lax.psum(kept, axis)


def trailing_product(column_panel, transposed):
    return jnp.einsum(
        "tan,sbn->tasb",
        column_panel,
        transposed,
        precision=lax.Precision.HIGHEST,
        preferred_element_type=jnp.float32,
    )


def shards(matrix):
    local_rows = matrix.shape[0]
    local_cols = matrix.shape[3]
    blocks = matrix.reshape(local_rows, NB, local_cols, NB)
    row_count = lax.axis_size("row")
    column_count = lax.axis_size("col")
    group_size = row_count // column_count
    row_place = lax.axis_index("row")
    column_place = lax.axis_index("col")
    tile_rows = jnp.arange(local_rows, dtype=jnp.int32) * row_count + row_place
    tile_columns = jnp.arange(local_cols, dtype=jnp.int32) * column_count + column_place
    anchor = jnp.int32(0)
    for step in range(STEPS):
        root_row = step % row_count
        factor_local_row = step // row_count
        root_col = step % column_count
        factor_local_col = step // column_count
        corner = blocks[factor_local_row, :, factor_local_col, :]
        owner = (row_place == root_row) & (column_place == root_col)
        identity = jnp.eye(NB, dtype=jnp.float32)
        chosen = jnp.where(owner, corner, identity)
        factor_local = jnp.linalg.cholesky(chosen)
        factor_diag_block = spread(factor_local, "row", root_row)
        source = blocks[:, :, factor_local_col, :]
        solved = jax.scipy.linalg.solve_triangular(
            factor_diag_block, source.reshape(local_rows * NB, NB).T, lower=True
        ).T
        solved = solved.reshape(local_rows, NB, NB)
        panel_local = jnp.where((tile_rows > step)[:, None, None], solved, 0.0)
        factor_column_panel = spread(panel_local, "col", root_col)
        empty = jnp.zeros((local_rows, group_size, NB, NB), jnp.float32)
        slot_index = row_place // column_count
        holder = row_place % column_count == column_place
        contribution = jnp.where(holder, factor_column_panel, 0.0)
        filled = lax.dynamic_update_slice(
            empty, contribution[:, None], (anchor, slot_index, anchor, anchor)
        )
        gathered = lax.psum(filled, "row")
        transposed = gathered.reshape(local_cols, NB, NB)
        diag_block, column_panel, transposed = (factor_diag_block, factor_column_panel, transposed)
        write_blocks = blocks
        local_row = step // row_count
        local_col = step // column_count
        column_now = write_blocks[:, :, local_col, :]
        owns_col = column_place == step % column_count
        row_after = (tile_rows > step)[:, None, None]
        row_hit = (tile_rows == step)[:, None, None]
        new_column = jnp.where(
            row_after, column_panel, jnp.where(row_hit, diag_block[None], column_now)
        )
        new_column = jnp.where(owns_col, new_column, column_now)
        write_blocks = write_blocks.at[:, :, local_col, :].set(new_column)
        row_now = write_blocks[local_row]
        owns_row = row_place == step % row_count
        zero_cols = (tile_columns > step)[None, :, None]
        new_row = jnp.where(owns_row & zero_cols, 0.0, row_now)
        blocks = write_blocks.at[local_row].set(new_row)
        blocks = blocks - trailing_product(column_panel, transposed)
    return blocks.reshape(matrix.shape)


def solution(mesh):
    in_specs = (P(None, "row", None, None, "col", None),)
    out_specs = P(None, "row", None, None, "col", None)
    return jax.shard_map(shards, mesh=mesh, in_specs=in_specs, out_specs=out_specs, check_vma=False)
```

profile of v0, /device:TPU:0, one launch (start us, length us, event | category | flops | bytes accessed | tf_op | source)
XLA Modules:
  0.0 1563.9 jit_solution(13661579687502120736)
XLA Ops:
  6.5 78.2 %copy.17 = f32[4,1,512,8,1,512]{2,5,3,0,4,1:T(8,128)} copy(f32[4,1,512,8,1,512]{5,4,3,2,1,0:T(1,128)} %param.12) | data formatting | bytes 67108864 | tf_op args[0]
  87.9 11.7 cholesky.286
  99.7 9.8 custom-call.27
  110.3 11.7 cholesky.305
  122.0 10.0 custom-call.28
  132.7 11.7 cholesky.326
  145.2 9.8 custom-call.29
  155.6 11.7 cholesky.343
  182.8 78.7 %copy.42 = f32[4,1,512,8,1,512]{2,5,0,3,1,4:T(8,128)} copy(f32[4,1,512,8,1,512]{5,4,3,2,1,0:T(1,128)} %param.12) | data formatting | bytes 67108864 | tf_op jit(solution)/shard_map/reshape | solution.py:28
  272.9 7.6 while.8
  280.5 39.3 %custom-call.30 = f32[4,128,128]{1,2,0:T(8,128)S(1)} custom-call(f32[4,128,128]{2,1,0:T(8,128)S(1)} %get-tuple-element.69), custom_call_target="InvertDiagBlocksLowerTriangular" | custom-call | tf_op jit(solution)/shard_map/jit(_solve_triangular)/triangular_solve | solution.py:49
  355.9 88.4 %all-reduce.10.cloned.1.call-done = f32[4,512,512]{1,2,0:T(8,128)} async-done(((f32[4,512,512]{1,2,0:T(8,128)}), f32[4,512,512]{1,2,0:T(8,128)}) %all-reduce.10.cloned.1.call-update) | async-done | bytes 4194320 | tf_op jit(solution)/shard_map/psum | solution.py:12
  462.3 6.8 bitcast_dynamic-update-slice_fusion.2
  469.2 8.3 fusion.1
  477.5 253.1 %all-reduce.12.cloned.1.call-done = f32[8,512,512]{2,1,0:T(8,128)} async-done(((f32[8,512,512]{2,1,0:T(8,128)}), f32[8,512,512]{2,1,0:T(8,128)}) %all-reduce.12.cloned.1.call-update) | async-done | bytes 8388624 | tf_op jit(solution)/shard_map/psum | solution.py:62
  730.6 63.0 %convolution_subtract_fusion = f32[4,512,8,512]{1,3,2,0:T(8,128)} fusion(f32[4,512,8,512]{1,3,2,0:T(8,128)} %fusion.1, f32[8,512,512]{2,1,0:T(8,128)} %all-reduce.12.cloned.1.call-done, f32[4,512,512]{1,2,0:T(8,128)} %all-reduce.10.cloned.1.call-done), kind=kOutput, calls=%fused_computation.5 | convolution fusion | flops 51547996160 | bytes 79691776 | tf_op jit(solution)/shard_map/tan,sbn->tasb/dot_general | solution.py:16
  796.7 11.7 cholesky.358
  808.6 9.8 custom-call.31
  819.1 11.7 cholesky.377
  832.2 10.2 custom-call.32
  843.0 11.7 cholesky.398
  855.5 9.8 custom-call.33
  865.9 11.7 cholesky.415
  894.3 65.6 %all-reduce.14.cloned.1.call-done = f32[512,512]{1,0:T(8,128)} async-done(((f32[512,512]{1,0:T(8,128)}), f32[512,512]{1,0:T(8,128)}) %all-reduce.14.cloned.1.call-update) | async-done | bytes 1048592 | tf_op jit(solution)/shard_map/psum | solution.py:12
  961.2 7.8 while.9
  969.0 39.3 %custom-call.34 = f32[4,128,128]{1,2,0:T(8,128)S(1)} custom-call(f32[4,128,128]{2,1,0:T(8,128)S(1)} %get-tuple-element.70), custom_call_target="InvertDiagBlocksLowerTriangular" | custom-call | tf_op jit(solution)/shard_map/jit(_solve_triangular)/triangular_solve | solution.py:49
  1044.2 85.2 %all-reduce.16.cloned.1.call-done = f32[4,512,512]{1,2,0:T(8,128)} async-done(((f32[4,512,512]{1,2,0:T(8,128)}), f32[4,512,512]{1,2,0:T(8,128)}) %all-reduce.16.cloned.1.call-update) | async-done | bytes 4194320 | tf_op jit(solution)/shard_map/psum | solution.py:12
  1147.6 6.8 fusion.6
  1154.4 8.3 fusion
  1162.7 253.0 %all-reduce.18.cloned.1.call-done = f32[8,512,512]{2,1,0:T(8,128)} async-done(((f32[8,512,512]{2,1,0:T(8,128)}), f32[8,512,512]{2,1,0:T(8,128)}) %all-reduce.18.cloned.1.call-update) | async-done | bytes 8388624 | tf_op jit(solution)/shard_map/psum | solution.py:62
  1415.8 62.8 %subtract_bitcast_fusion = f32[4,1,512,8,1,512]{2,5,3,0,4,1:T(8,128)} fusion(f32[4,512,8,512]{1,3,2,0:T(8,128)} %fusion, f32[8,512,512]{2,1,0:T(8,128)} %all-reduce.18.cloned.1.call-done, f32[4,512,512]{1,2,0:T(8,128)} %all-reduce.16.cloned.1.call-done), kind=kOutput, calls=%fused_computation.4 | convolution fusion | flops 51547996160 | bytes 79691776 | tf_op jit(solution)/shard_map/tan,sbn->tasb/dot_general | solution.py:16
  1478.5 78.2 %copy.37 = f32[4,1,512,8,1,512]{5,4,3,2,1,0:T(1,128)} copy(f32[4,1,512,8,1,512]{2,5,3,0,4,1:T(8,128)} %subtract_bitcast_fusion) | data formatting | bytes 67108864 | tf_op jit(solution)/shard_map/reshape | solution.py:83
  (140 shorter events, 165.6 us)
Async XLA Ops:
  6.5 264.9 %all-reduce.8.cloned.1.call-start = ((), (), s32[]{:S(2)}) async-start(), calls=%async_computation | async-start | bytes 2097152 | tf_op jit(solution)/shard_map/psum | solution.py:12
  182.8 261.4 %all-reduce.10.cloned.1.call-start = ((), (), s32[]{:S(2)}) async-start(), calls=%async_computation.1 | async-start | bytes 8388608 | tf_op jit(solution)/shard_map/psum | solution.py:12
  319.8 6.6 copy-start.2
  355.8 374.8 %all-reduce.12.cloned.1.call-start = ((), (), s32[]{:S(2)}) async-start(), calls=%async_computation.2 | async-start | bytes 16777216 | tf_op jit(solution)/shard_map/psum | solution.py:62
  454.1 4.3 copy-start.1
  460.8 1.2 copy-start.4
  460.8 499.0 %all-reduce.14.cloned.1.call-start = ((), (), s32[]{:S(2)}) async-start(), calls=%async_computation.3 | async-start | bytes 2097152 | tf_op jit(solution)/shard_map/psum | solution.py:12
  882.2 247.2 %all-reduce.16.cloned.1.call-start = ((), (), s32[]{:S(2)}) async-start(), calls=%async_computation.4 | async-start | bytes 8388608 | tf_op jit(solution)/shard_map/psum | solution.py:12
  1008.4 6.6 copy-start.3
  1044.2 371.6 %all-reduce.18.cloned.1.call-start = ((), (), s32[]{:S(2)}) async-start(), calls=%async_computation.5 | async-start | bytes 16777216 | tf_op jit(solution)/shard_map/psum | solution.py:62
  1139.3 4.3 copy-start
  1146.0 1.2 copy-start.5
Sparse Core Ops, SparseCore 0:
  182.9 81.0 all-reduce.7
  355.9 88.2 all-reduce.9
  460.9 269.6 all-reduce.11
  882.3 77.4 all-reduce.13
  1044.3 85.0 all-reduce.15
  1146.1 269.5 all-reduce.17
where the time goes:
time: 1580 us; the launch traced here: 1560 us
  waiting for transfers between devices  745 us (47%)
  local copies, waits for them, and re-layouts  321 us (20%)
  other arithmetic  302 us (19%)
  matrix products  165 us (10%)
  between operations  30 us (2%)
    psum x2, waiting for transfers between devices, shards(): gathered = lax.psum(filled, 'row')  506 us
    psum x4, waiting for transfers between devices, spread(): return lax.psum(kept, axis)  239 us
    another operation x29, other arithmetic, shards(): factor_local = jnp.linalg.cholesky(chosen)  158 us
    dot_general x2, matrix products, trailing_product(): jnp.einsum('tan,sbn->tasb', column_panel, transposed, precision=lax.Preci...  126 us
    another operation x5, other arithmetic, shards(): jax.scipy.linalg.solve_triangular(factor_diag_block, source.reshape(local...  81.3 us
    unnamed x13, local copies, waits for them, and re-layouts  80.5 us
    reshape x1, local copies, waits for them, and re-layouts, shards(): blocks = matrix.reshape(local_rows, NB, local_cols, NB)  78.7 us
    reshape x1, local copies, waits for them, and re-layouts, shards(): return blocks.reshape(matrix.shape)  78.2 us
  transfers between devices with their start and end apart: 6, of which 5 were waited for; matrix products, arithmetic and copies ran while one was open for 8% of the time, Pallas kernels for 0%

commit v1 on v0

--- a/solution.py
+++ b/solution.py
@@ -59,7 +59,11 @@
         filled = lax.dynamic_update_slice(
             empty, contribution[:, None], (anchor, slot_index, anchor, anchor)
         )
-        gathered = lax.psum(filled, "row")
+        gathered = filled
+        for hop in (1, 2, 4):
+            gathered = gathered + lax.ppermute(
+                gathered, "row", [(dev, dev ^ hop) for dev in range(8)]
+            )
         transposed = gathered.reshape(local_cols, NB, NB)
         diag_block, column_panel, transposed = (factor_diag_block, factor_column_panel, transposed)
         write_blocks = blocks

time: 1580 us -> 2530 us (1.60)
  waiting for transfers between devices: 745 us -> 1650 us
  other arithmetic: 302 us -> 341 us
    ppermute x0 -> x6, waiting for transfers between devices: none -> 1410 us  [shards(): lax.ppermute(gathered, 'row', [(dev, dev ^ hop) for dev in range(8)])]
    psum x2 -> x0, waiting for transfers between devices: 506 us -> none  [shards(): gathered = lax.psum(filled, 'row')]
    add x0 -> x6, other arithmetic: none -> 46.9 us  [shards(): gathered + lax.ppermute(gathered, 'row', [(dev, dev ^ hop) for dev in ran...]
    unnamed x13 -> x17, local copies, waits for them, and re-layouts: 80.5 us -> 86.9 us
  transfers between devices with their start and end apart: 6 -> 10, of which waited for: 5 -> 9; matrix products, arithmetic and copies ran while one was open for 8% -> 5% of each run, Pallas kernels for 0% -> 0%
where the time goes in v1:
time: 2530 us; the launch traced here: 2510 us
  waiting for transfers between devices  1650 us (65%)
  other arithmetic  341 us (13%)
  local copies, waits for them, and re-layouts  326 us (13%)
  matrix products  166 us (7%)
    ppermute x6, waiting for transfers between devices, shards(): lax.ppermute(gathered, 'row', [(dev, dev ^ hop) for dev in range(8)])  1410 us
    psum x4, waiting for transfers between devices, spread(): return lax.psum(kept, axis)  241 us
    another operation x29, other arithmetic, shards(): factor_local = jnp.linalg.cholesky(chosen)  158 us
    dot_general x2, matrix products, trailing_product(): jnp.einsum('tan,sbn->tasb', column_panel, transposed, precision=lax.Preci...  126 us
    unnamed x17, local copies, waits for them, and re-layouts  86.9 us
    another operation x5, other arithmetic, shards(): jax.scipy.linalg.solve_triangular(factor_diag_block, source.reshape(local...  81.3 us
    reshape x1, local copies, waits for them, and re-layouts, shards(): blocks = matrix.reshape(local_rows, NB, local_cols, NB)  78.7 us
    reshape x1, local copies, waits for them, and re-layouts, shards(): return blocks.reshape(matrix.shape)  78.2 us
  transfers between devices with their start and end apart: 10, of which 9 were waited for; matrix products, arithmetic and copies ran while one was open for 5% of the time, Pallas kernels for 0%

profile of v1, /device:TPU:0, one launch (start us, length us, event | category | flops | bytes accessed | tf_op | source)
XLA Modules:
  0.0 2510.5 jit_solution(17131408131632243650)
XLA Ops:
  6.5 78.2 %copy.15 = f32[4,1,512,8,1,512]{2,5,3,0,4,1:T(8,128)} copy(f32[4,1,512,8,1,512]{5,4,3,2,1,0:T(1,128)} %param.12) | data formatting | bytes 67108864 | tf_op args[0]
  87.9 11.7 cholesky.286
  110.3 11.7 cholesky.305
  122.0 10.2 custom-call.28
  133.0 11.7 cholesky.326
  155.1 11.7 cholesky.343
  172.8 78.7 %copy.40 = f32[4,1,512,8,1,512]{2,5,0,3,1,4:T(8,128)} copy(f32[4,1,512,8,1,512]{5,4,3,2,1,0:T(1,128)} %param.12) | data formatting | bytes 67108864 | tf_op jit(solution)/shard_map/reshape | solution.py:28
  270.4 39.3 %custom-call.30 = f32[4,128,128]{1,2,0:T(8,128)S(1)} custom-call(f32[4,128,128]{2,1,0:T(8,128)S(1)} %get-tuple-element.69), custom_call_target="InvertDiagBlocksLowerTriangular" | custom-call | tf_op jit(solution)/shard_map/jit(_solve_triangular)/triangular_solve | solution.py:49
  345.8 88.4 %all-reduce.8.cloned.1.call-done = f32[4,512,512]{1,2,0:T(8,128)} async-done(((f32[4,512,512]{1,2,0:T(8,128)}), f32[4,512,512]{1,2,0:T(8,128)}) %all-reduce.8.cloned.1.call-update) | async-done | bytes 4194320 | tf_op jit(solution)/shard_map/psum | solution.py:12
  438.5 180.4 %collective-permute-done = f32[4,2,512,512]{2,3,0,1:T(8,128)S(1)} collective-permute-done((f32[4,2,512,512]{2,3,0,1:T(8,128)S(1)}, f32[4,2,512,512]{2,3,0,1:T(8,128)S(1)}, u32[]{:S(2)}, u32[]{:S(2)}) %collective-permute-start) | collective-permute-done | bytes 8388640 | tf_op jit(solution)/shard_map/ppermute | solution.py:64
  624.9 179.6 %collective-permute-done.1 = f32[4,2,512,512]{2,3,0,1:T(8,128)} collective-permute-done((f32[4,2,512,512]{2,3,0,1:T(8,128)S(1)}, f32[4,2,512,512]{2,3,0,1:T(8,128)}, u32[]{:S(2)}, u32[]{:S(2)}) %collective-permute-start.1) | collective-permute-done | bytes 8388640 | tf_op jit(solution)/shard_map/ppermute | solution.py:64
  804.5 11.1 add.117
  833.5 343.2 %collective-permute-done.2 = f32[4,2,512,512]{2,3,0,1:T(8,128)} collective-permute-done((f32[4,2,512,512]{2,3,0,1:T(8,128)}, f32[4,2,512,512]{2,3,0,1:T(8,128)}, u32[]{:S(2)}, u32[]{:S(2)}) %collective-permute-start.2) | collective-permute-done | bytes 8388640 | tf_op jit(solution)/shard_map/ppermute | solution.py:64
  1176.7 11.1 add.118
  1187.8 10.0 copy.23
  1197.8 63.0 %convolution_subtract_fusion = f32[4,512,8,512]{1,3,2,0:T(8,128)} fusion(f32[4,512,8,512]{1,3,2,0:T(8,128)} %fusion.1, f32[8,512,512,1]{2,1,0,3:T(8,128)} %bitcast.188, f32[4,512,512]{1,2,0:T(8,128)} %all-reduce.8.cloned.1.call-done), kind=kOutput, calls=%fused_computation.5 | convolution fusion | flops 51547996160 | bytes 79691776 | tf_op jit(solution)/shard_map/tan,sbn->tasb/dot_general | solution.py:16
  1264.0 11.7 cholesky.358
  1286.4 11.7 cholesky.377
  1298.1 10.3 custom-call.32
  1309.0 11.7 cholesky.398
  1331.2 11.7 cholesky.415
  1361.6 67.4 %all-reduce.10.cloned.1.call-done = f32[512,512]{1,0:T(8,128)} async-done(((f32[512,512]{1,0:T(8,128)}), f32[512,512]{1,0:T(8,128)}) %all-reduce.10.cloned.1.call-update) | async-done | bytes 1048592 | tf_op jit(solution)/shard_map/psum | solution.py:12
  1438.6 39.3 %custom-call.34 = f32[4,128,128]{1,2,0:T(8,128)S(1)} custom-call(f32[4,128,128]{2,1,0:T(8,128)S(1)} %get-tuple-element.70), custom_call_target="InvertDiagBlocksLowerTriangular" | custom-call | tf_op jit(solution)/shard_map/jit(_solve_triangular)/triangular_solve | solution.py:49
  1513.9 85.2 %all-reduce.12.cloned.1.call-done = f32[4,512,512]{1,2,0:T(8,128)} async-done(((f32[4,512,512]{1,2,0:T(8,128)}), f32[4,512,512]{1,2,0:T(8,128)}) %all-reduce.12.cloned.1.call-update) | async-done | bytes 4194320 | tf_op jit(solution)/shard_map/psum | solution.py:12
  1603.5 180.4 %collective-permute-done.3 = f32[4,2,512,512]{2,3,0,1:T(8,128)S(1)} collective-permute-done((f32[4,2,512,512]{2,3,0,1:T(8,128)S(1)}, f32[4,2,512,512]{2,3,0,1:T(8,128)S(1)}, u32[]{:S(2)}, u32[]{:S(2)}) %collective-permute-start.3) | collective-permute-done | bytes 8388640 | tf_op jit(solution)/shard_map/ppermute | solution.py:64
  1789.9 179.6 %collective-permute-done.4 = f32[4,2,512,512]{2,3,0,1:T(8,128)} collective-permute-done((f32[4,2,512,512]{2,3,0,1:T(8,128)S(1)}, f32[4,2,512,512]{2,3,0,1:T(8,128)}, u32[]{:S(2)}, u32[]{:S(2)}) %collective-permute-start.4) | collective-permute-done | bytes 8388640 | tf_op jit(solution)/shard_map/ppermute | solution.py:64
  1969.5 11.1 add.120
  1998.5 343.2 %collective-permute-done.5 = f32[4,2,512,512]{2,3,0,1:T(8,128)} collective-permute-done((f32[4,2,512,512]{2,3,0,1:T(8,128)}, f32[4,2,512,512]{2,3,0,1:T(8,128)}, u32[]{:S(2)}, u32[]{:S(2)}) %collective-permute-start.5) | collective-permute-done | bytes 8388640 | tf_op jit(solution)/shard_map/ppermute | solution.py:64
  2341.7 11.1 add.121
  2352.8 9.9 copy.32
  2362.7 62.9 %subtract_bitcast_fusion = f32[4,1,512,8,1,512]{2,5,3,0,4,1:T(8,128)} fusion(f32[4,512,8,512]{1,3,2,0:T(8,128)} %fusion, f32[8,512,512,1]{2,1,0,3:T(8,128)} %bitcast.189, f32[4,512,512]{1,2,0:T(8,128)} %all-reduce.12.cloned.1.call-done), kind=kOutput, calls=%fused_computation.4 | convolution fusion | flops 51547996160 | bytes 79691776 | tf_op jit(solution)/shard_map/tan,sbn->tasb/dot_general | solution.py:16
  2425.6 78.2 %copy.35 = f32[4,1,512,8,1,512]{5,4,3,2,1,0:T(1,128)} copy(f32[4,1,512,8,1,512]{2,5,3,0,4,1:T(8,128)} %subtract_bitcast_fusion) | data formatting | bytes 67108864 | tf_op jit(solution)/shard_map/reshape | solution.py:87
  (154 shorter events, 241.3 us)
Async XLA Ops:
  6.5 254.9 %all-reduce.6.cloned.1.call-start = ((), (), s32[]{:S(2)}) async-start(), calls=%async_computation | async-start | bytes 2097152 | tf_op jit(solution)/shard_map/psum | solution.py:12
  172.8 261.4 %all-reduce.8.cloned.1.call-start = ((), (), s32[]{:S(2)}) async-start(), calls=%async_computation.1 | async-start | bytes 8388608 | tf_op jit(solution)/shard_map/psum | solution.py:12
  309.8 6.6 copy-start.4
  345.7 1083.3 %all-reduce.10.cloned.1.call-start = ((), (), s32[]{:S(2)}) async-start(), calls=%async_computation.2 | async-start | bytes 2097152 | tf_op jit(solution)/shard_map/psum | solution.py:12
  434.2 2.2 copy-start
  437.0 181.9 %collective-permute-start = (f32[4,2,512,512]{2,3,0,1:T(8,128)S(1)}, f32[4,2,512,512]{2,3,0,1:T(8,128)S(1)}, u32[]{:S(2)}, u32[]{:S(2)}) collective-permute-start(f32[4,2,512,512]{2,3,0,1:T(8,128)S(1)} %bitcast_dynamic-update-slice_fusion.4), channel_id=1, source_target_pairs={{0,4},{4,0},{8,12},{12,8},{16,20},{20,16},{24,28},{28,24},{1,5},{5... | collective-permute-start | bytes 25165832 | tf_op jit(solution)/shard_map/ppermute | solution.py:64
  620.2 3.2 copy-start.3
  623.4 194.6 %copy-start.6 = (f32[512,512]{1,0:T(8,128)S(1)}, f32[512,512]{1,0:T(8,128)}, u32[]{:S(2)}) copy-start(f32[512,512]{1,0:T(8,128)} %all-reduce.6.cloned.1.call-done) | copy-start | bytes 3145732
  623.4 181.1 %collective-permute-start.1 = (f32[4,2,512,512]{2,3,0,1:T(8,128)S(1)}, f32[4,2,512,512]{2,3,0,1:T(8,128)}, u32[]{:S(2)}, u32[]{:S(2)}) collective-permute-start(f32[4,2,512,512]{2,3,0,1:T(8,128)S(1)} %fusion.8), channel_id=1, source_target_pairs={{0,8},{4,12},{8,0},{12,4},{16,24},{20,28},{24,16},{28,20},{1,9},{5... | collective-permute-start | bytes 25165832 | tf_op jit(solution)/shard_map/ppermute | solution.py:64
  815.6 361.1 %collective-permute-start.2 = (f32[4,2,512,512]{2,3,0,1:T(8,128)}, f32[4,2,512,512]{2,3,0,1:T(8,128)}, u32[]{:S(2)}, u32[]{:S(2)}) collective-permute-start(f32[4,2,512,512]{2,3,0,1:T(8,128)} %add.117), channel_id=1, source_target_pairs={{0,16},{4,20},{8,24},{12,28},{16,0},{20,4},{24,8},{28,12},{1,17},{... | collective-permute-start | bytes 25165832 | tf_op jit(solution)/shard_map/ppermute | solution.py:64
  1349.5 249.6 %all-reduce.12.cloned.1.call-start = ((), (), s32[]{:S(2)}) async-start(), calls=%async_computation.3 | async-start | bytes 8388608 | tf_op jit(solution)/shard_map/psum | solution.py:12
  1477.9 6.6 copy-start.5
  1599.2 2.2 copy-start.1
  1601.9 181.9 %collective-permute-start.3 = (f32[4,2,512,512]{2,3,0,1:T(8,128)S(1)}, f32[4,2,512,512]{2,3,0,1:T(8,128)S(1)}, u32[]{:S(2)}, u32[]{:S(2)}) collective-permute-start(f32[4,2,512,512]{2,3,0,1:T(8,128)S(1)} %bitcast_dynamic-update-slice_fusion.3), channel_id=1, source_target_pairs={{0,4},{4,0},{8,12},{12,8},{16,20},{20,16},{24,28},{28,24},{1,5},{5... | collective-permute-start | bytes 25165832 | tf_op jit(solution)/shard_map/ppermute | solution.py:64
  1785.2 3.2 copy-start.2
  1788.4 194.6 %copy-start.7 = (f32[512,512]{1,0:T(8,128)S(1)}, f32[512,512]{1,0:T(8,128)}, u32[]{:S(2)}) copy-start(f32[512,512]{1,0:T(8,128)} %all-reduce.10.cloned.1.call-done) | copy-start | bytes 3145732
  1788.4 181.1 %collective-permute-start.4 = (f32[4,2,512,512]{2,3,0,1:T(8,128)S(1)}, f32[4,2,512,512]{2,3,0,1:T(8,128)}, u32[]{:S(2)}, u32[]{:S(2)}) collective-permute-start(f32[4,2,512,512]{2,3,0,1:T(8,128)S(1)} %fusion.7), channel_id=1, source_target_pairs={{0,8},{4,12},{8,0},{12,4},{16,24},{20,28},{24,16},{28,20},{1,9},{5... | collective-permute-start | bytes 25165832 | tf_op jit(solution)/shard_map/ppermute | solution.py:64
  1980.6 361.1 %collective-permute-start.5 = (f32[4,2,512,512]{2,3,0,1:T(8,128)}, f32[4,2,512,512]{2,3,0,1:T(8,128)}, u32[]{:S(2)}, u32[]{:S(2)}) collective-permute-start(f32[4,2,512,512]{2,3,0,1:T(8,128)} %add.120), channel_id=1, source_target_pairs={{0,16},{4,20},{8,24},{12,28},{16,0},{20,4},{24,8},{28,12},{1,17},{... | collective-permute-start | bytes 25165832 | tf_op jit(solution)/shard_map/ppermute | solution.py:64
Sparse Core Ops, SparseCore 0:
  172.9 81.0 all-reduce.5
  345.9 88.2 all-reduce.7
  1349.7 79.2 all-reduce.9
  1514.1 85.0 all-reduce.11
